TPU v7x, 32 devices: a whole 2x2x4 slice. The times are simulated.
32 devices in a mesh: leaf: 32 (over z, y, x, core).
Axes of the slice: x: 2, y: 2, z: 4, core: 2. Of those that a mesh axis runs over, the one named last changes fastest.
Arguments:
- panels: bfloat16 [64, 64, 256], P('leaf'), may hold values from -6 to 6
- basis: bfloat16 [64, 64, 256], P('leaf'), may hold values from -0.375 to 0.375
- transfer: bfloat16 [64, 64, 64], P('leaf'), may hold values from -0.25 to 0.25
- near_blocks: bfloat16 [64, 27, 256, 256], P('leaf'), may hold values from -0.078125 to 0.078125
- coupling: bfloat16 [2, 343, 4096], replicated, may hold values from -0.0546875 to 0.0546875
- near_list: int32 [64, 27], P('leaf'), may hold values from -1 to 63, as said below
Outputs:
- product: bfloat16 [64, 64, 256], P('leaf')
Inputs may be any that keep to these rules, and one draw needn't show every extreme that they name: `near_list`: row i lists, in an order of no meaning, leaf i and the leaves whose grid positions differ from it by at most one in each coordinate; -1 fills the other slots.
All inputs are finite; a program needn't handle non-finite values.
Results may differ from a plain program's by a relative error of at most 0.0035.
Values may be sent and summed in bfloat16 or wider, within the bound.
A program may use at most 192 MiB of HBM per device.

v0:
```python
import functools

import jax
import jax.numpy as jnp
from jax import lax
from jax.experimental import pallas as pl
from jax.experimental.pallas import tpu as pltpu
from jax.sharding import PartitionSpec as P

MESH = pl.DeviceIdType.MESH
F32 = jnp.float32
BF16 = jnp.bfloat16
REACH = 3
SPAN = 2 * REACH + 1
TN = (((0,), (0,)), ((), ()))
NT = (((1,), (1,)), ((), ()))
OFFSETS = [(a, b, c) for a in (-1, 0, 1) for b in (-1, 0, 1) for c in (-1, 0, 1)]


def axis_bits(first, bit_count):
    return [[b for b in range(bit_count) if (b + first) % 3 == a] for a in range(3)]


def coords_of(index, bits):
    return [
        sum(((index // 2**b) % 2) * 2**p for p, b in enumerate(bits[a])) + index * 0
        for a in range(3)
    ]


def index_of(coords, bits):
    return sum(((coords[a] // 2**p) % 2) * 2**b for a in range(3) for p, b in enumerate(bits[a]))


def inside(coords, bits):
    ok = None
    for a in range(3):
        here = (coords[a] >= 0) & (coords[a] < 2 ** len(bits[a]))
        ok = here if ok is None else ok & here
    return ok


def far_mats(targets, bit_count, coupling, level, spread, mats):
    half = coupling.shape[1] // 2
    count = 2 ** (bit_count - 3)

    @pl.loop(0, min(count, 27))
    def _(i):
        upper, _, ok = candidate(targets[0], bit_count, i)
        columns = []
        for l, target in enumerate(targets):
            column = []
            for h in range(8):
                d = [2 * upper[a] + (h >> a & 1) - target[a] for a in range(3)]
                apart = (jnp.abs(d[0]) > 1) | (jnp.abs(d[1]) > 1) | (jnp.abs(d[2]) > 1)
                use = ok & apart
                code = (SPAN * (d[0] + REACH) + d[1] + REACH) * SPAN + d[2] + REACH
                code = jnp.where(use, code, 0)
                at = (l * 8 + h) * 2 * half
                spread[at : at + 2 * half, :] = coupling[code].astype(F32)
                mat = spread[pl.ds(at + level, half, stride=2), :]
                mat = mat * jnp.where(use, 1.0, 0.0).astype(F32)
                column.append(mat.astype(BF16))
            columns.append(jnp.concatenate(column, axis=0))
        mats[i] = jnp.concatenate(columns, axis=1) if len(columns) > 1 else columns[0]


def candidate(target, bit_count, i):
    bits = axis_bits(0, bit_count - 3)
    home = [c // 2 for c in target]
    if 2 ** (bit_count - 3) <= 27:
        upper = coords_of(i, bits)
        ok = None
        for a in range(3):
            near = jnp.abs(upper[a] - home[a]) <= 1
            ok = near if ok is None else ok & near
        return upper, i, ok
    upper = [home[0] + i // 9 - 1, home[1] + (i // 3) % 3 - 1, home[2] + i % 3 - 1]
    ok = inside(upper, bits)
    return upper, jnp.where(ok, index_of([jnp.maximum(u, 0) for u in upper], bits), 0), ok


def far_sum(targets, bit_count, stacked, mats, rank):
    depth = 8 * rank // 2
    count = 2 ** (bit_count - 3)

    def step(i, total):
        _, q, _ = candidate(targets[0], bit_count, i)
        rows = pl.ds(pl.multiple_of(q * depth, depth), depth)
        return total + lax.dot_general(stacked[rows, :], mats[i], TN, preferred_element_type=F32)

    start = jnp.zeros((2 * rank, 2 * rank * len(targets)), F32)
    total = lax.fori_loop(0, min(count, 27), step, start)
    result = []
    for l in range(len(targets)):
        part = total[:, 2 * rank * l : 2 * rank * (l + 1)]
        result.append(part[:rank, :rank] + part[rank:, rank:])
    return result


def kernel(
    n,
    panels,
    basis,
    transfer,
    blocks_hbm,
    coupling_hbm,
    near_list,
    out,
    all_panels,
    blocks,
    coupling,
    spread,
    mats0,
    mats1,
    coefs,
    parts,
    clusters,
    blocks_sem,
    coupling_sem,
    panel_send,
    panel_recv,
    coef_send,
    coef_recv,
    relay_send,
    relay_recv,
    part_send,
    part_recv,
    cluster_send,
    cluster_recv,
):
    leaf_dev, columns, points = panels.shape
    rank = basis.shape[1]
    slots = near_list.shape[1]
    half = rank // 2
    low_bits = leaf_dev.bit_length() - 1
    dev_bits = n.bit_length() - 1
    bit_count = low_bits + dev_bits
    group = 8 // leaf_dev
    groups = n // group
    chips = n // 2
    own_rows = leaf_dev * half
    me = lax.axis_index("leaf")
    chip, core = me // 2, me % 2
    mate = chip * 2 + 1 - core

    loads = [pltpu.make_async_copy(coupling_hbm, coupling, coupling_sem)]
    cut = slots // 3 if slots % 3 == 0 else slots
    for l in range(leaf_dev):
        for i in range(slots // cut):
            rows = pl.ds(i * cut, cut)
            loads.append(
                pltpu.make_async_copy(
                    blocks_hbm.at[l, rows],
                    blocks.at[l, rows],
                    blocks_sem.at[l * (slots // cut) + i],
                )
            )
    for load in loads:
        load.start()

    barrier = pltpu.get_barrier_semaphore()

    @pl.loop(1, n)
    def _(j):
        pl.semaphore_signal(
            barrier, inc=1, device_id=(lax.rem(me + j, n),), device_id_type=MESH
        )

    row = lax.broadcasted_iota(jnp.int32, (rank, rank), 0)
    col = lax.broadcasted_iota(jnp.int32, (rank, rank), 1)
    source = 2 * (row % half) + row // half
    order = jnp.where(col == source, 1.0, 0.0).astype(BF16)
    term = jnp.zeros((rank, columns), F32)
    for l in range(leaf_dev):
        flat = lax.dot_general(
            basis[l], panels[l], NT, preferred_element_type=F32
        ).astype(BF16)
        mixed = jnp.dot(order, flat, preferred_element_type=F32).astype(BF16)
        packed = jnp.concatenate([mixed[:half], mixed[half:]], axis=1)
        at = pl.multiple_of(me * own_rows, own_rows) + l * half
        coefs[pl.ds(pl.multiple_of(at, half), half), :] = packed
        sent = lax.dot_general(
            order, transfer[l], NT, preferred_element_type=F32
        ).astype(BF16)
        term = term + jnp.dot(sent, flat, preferred_element_type=F32)
    parts[0] = jnp.concatenate([term[:half], term[half:]], axis=1)
    for l in range(leaf_dev):
        all_panels[me * leaf_dev + l] = panels[l]

    pl.semaphore_wait(barrier, n - 1)

    def own_block(device):
        return coefs.at[pl.ds(pl.multiple_of(device * own_rows, own_rows), own_rows), :]

    places = min(4, chips)
    columns_of_chips = chips // places
    line, place = chip // places, lax.rem(chip, places)

    def coef_device(j, k):
        from_line = lax.rem(line - j + columns_of_chips, columns_of_chips)
        from_place = lax.rem(place - k + places, places)
        return (from_line * places + from_place) * 2 + core

    def coef_copy(j, k):
        to_line = lax.rem(line + j, columns_of_chips) if k is None else line
        to_place = place if k is None else lax.rem(place + k, places)
        m = j * places + (0 if k is None else k)
        block = own_block(me) if k is None else own_block(coef_device(j, 0))
        return pltpu.make_async_remote_copy(
            src_ref=block,
            dst_ref=block,
            send_sem=coef_send.at[m],
            recv_sem=coef_recv.at[m],
            device_id=((to_line * places + to_place) * 2 + core,),
            device_id_type=MESH,
        )

    def relay_copy(m, device):
        return pltpu.make_async_remote_copy(
            src_ref=own_block(device),
            dst_ref=own_block(device),
            send_sem=relay_send.at[m],
            recv_sem=relay_recv.at[m],
            device_id=(mate,),
            device_id_type=MESH,
        )

    def part_copy(j):
        base = (me // group) * group
        return pltpu.make_async_remote_copy(
            src_ref=parts.at[0],
            dst_ref=parts.at[j],
            send_sem=part_send.at[j],
            recv_sem=part_recv.at[j],
            device_id=(base + lax.rem(me - base + j, group),),
            device_id_type=MESH,
        )

    def cluster_block(p):
        return clusters.at[pl.ds(pl.multiple_of(p * half, half), half), :]

    def cluster_copy(j, p):
        return pltpu.make_async_remote_copy(
            src_ref=cluster_block(p),
            dst_ref=cluster_block(p),
            send_sem=cluster_send.at[j],
            recv_sem=cluster_recv.at[j],
            device_id=(lax.rem(me + j * group, n),),
            device_id_type=MESH,
        )

    bits = axis_bits(low_bits, dev_bits)
    where = coords_of(me, bits)

    def hop_of(o):
        x, y, z = OFFSETS[o]
        return (0, y, 0) if y else (x, 0, 0) if x else (0, 0, z)

    def moved(offset):
        there = [where[a] + offset[a] for a in range(3)]
        ok = inside(there, bits)
        return ok, jnp.where(ok, index_of([jnp.maximum(v, 0) for v in there], bits), 0)

    def panel_copy(o, source, receiver):
        first, count = 0, leaf_dev
        if leaf_dev == 2 and OFFSETS[o][0] != 0:
            first, count = (1 if OFFSETS[o][0] > 0 else 0), 1
        rows = pl.ds(source * leaf_dev + first, count)
        owned = hop_of(o) == OFFSETS[o]
        return pltpu.make_async_remote_copy(
            src_ref=panels.at[pl.ds(first, count)] if owned else all_panels.at[rows],
            dst_ref=all_panels.at[rows],
            send_sem=panel_send.at[o],
            recv_sem=panel_recv.at[o],
            device_id=(receiver,),
            device_id_type=MESH,
        )

    def sends(o, act):
        hop = hop_of(o)
        ok, to = moved(hop)
        known, source = moved([h - e for h, e in zip(hop, OFFSETS[o])])

        @pl.when(ok & known)
        def _():
            act(panel_copy(o, source, to))

    def receives(o):
        known, source = moved([-e for e in OFFSETS[o]])

        @pl.when(known)
        def _():
            panel_copy(o, source, me).wait_recv()

    reach = [o for o in range(27) if OFFSETS[o] != (0, 0, 0)]
    along_z = [o for o in reach if not OFFSETS[o][0] and not OFFSETS[o][1]]
    along_x = [o for o in reach if OFFSETS[o][0] and not OFFSETS[o][1]]
    along_y = [o for o in reach if OFFSETS[o][1]]

    def start(copy):
        copy.start()

    for j in range(1, group):
        part_copy(j).start()
    for o in along_z:
        sends(o, start)

    @pl.loop(1, columns_of_chips)
    def _(j):
        coef_copy(j, None).start()

    relay_copy(0, me).start()
    for k in range(1, places):
        coef_copy(0, k).start()
    for o in along_x + along_y:
        if hop_of(o) == OFFSETS[o]:
            sends(o, start)

    for j in range(1, group):
        part_copy(j).wait_recv()
    mine = me // group
    total = parts[0]
    for j in range(1, group):
        total = total + parts[j]
    clusters[pl.ds(pl.multiple_of(mine * half, half), half), :] = total.astype(BF16)

    for o in along_z:
        receives(o)
        for later in along_x + along_y:
            before = [e - h for e, h in zip(OFFSETS[later], hop_of(later))]
            if tuple(before) == OFFSETS[o]:
                sends(later, start)

    @pl.loop(1, columns_of_chips)
    def _(j):
        coef_copy(j, None).wait_recv()
        for k in range(1, places):
            coef_copy(j, k).start()
        relay_copy(j * places, coef_device(j, 0)).start()

    @pl.loop(1, groups)
    def _(j):
        cluster_copy(j, mine).start()

    for o in along_x:
        receives(o)
        for later in along_y:
            before = [e - h for e, h in zip(OFFSETS[later], hop_of(later))]
            if tuple(before) == OFFSETS[o]:
                sends(later, start)

    @pl.loop(0, columns_of_chips)
    def _(j):
        for k in range(1, places):
            coef_copy(j, k).wait_recv()
            relay_copy(j * places + k, coef_device(j, k)).start()

    parent = coords_of(mine, axis_bits(0, bit_count - 3))
    leaf_bits = axis_bits(0, bit_count)
    targets = [coords_of(me * leaf_dev + l, leaf_bits) for l in range(leaf_dev)]
    loads[0].wait()
    far_mats([parent], bit_count - 3, coupling, 1, spread, mats1)
    far_mats(targets, bit_count, coupling, 0, spread, mats0)

    @pl.loop(0, chips)
    def _(m):
        relay_copy(m, me).wait_recv()

    leaf_far = far_sum(targets, bit_count, coefs, mats0, rank)

    @pl.loop(1, groups)
    def _(j):
        cluster_copy(j, mine).wait_recv()

    down = far_sum([parent], bit_count - 3, clusters, mats1, rank)[0].astype(BF16)
    far_terms = []
    for l in range(leaf_dev):
        far = leaf_far[l] + lax.dot_general(down, transfer[l], NT, preferred_element_type=F32)
        far_terms.append(jnp.dot(far.astype(BF16), basis[l], preferred_element_type=F32))

    for o in along_y:
        receives(o)
    for load in loads[1:]:
        load.wait()
    for l in range(leaf_dev):
        total = far_terms[l]
        for k in range(slots):
            j = near_list[l, k]
            block = all_panels[jnp.maximum(j, 0)]
            block = jnp.where(j >= 0, block, jnp.zeros_like(block))
            total = total + jnp.dot(block, blocks[l, k], preferred_element_type=F32)
        out[l] = total.astype(BF16)

    for j in range(1, group):
        part_copy(j).wait_send()

    @pl.loop(0, chips)
    def _(m):
        relay_copy(m, me).wait_send()

    @pl.loop(1, columns_of_chips)
    def _(j):
        coef_copy(j, None).wait_send()

    @pl.loop(0, columns_of_chips)
    def _(j):
        for k in range(1, places):
            coef_copy(j, k).wait_send()

    @pl.loop(1, groups)
    def _(j):
        cluster_copy(j, mine).wait_send()

    for o in reach:
        sends(o, lambda copy: copy.wait_send())


def per_device(panels, basis, transfer, near_blocks, coupling, near_list):
    n = lax.axis_size("leaf")
    leaf_dev, columns, points = panels.shape
    rank = basis.shape[1]
    slots = near_list.shape[1]
    shifts = coupling.shape[1]
    half = rank // 2
    leaves = n * leaf_dev
    coupling = coupling.transpose(1, 0, 2).reshape(shifts, 2, half, 2 * rank)
    coupling = coupling.transpose(0, 2, 1, 3).reshape(shifts, rank, 2 * rank)
    group = 8 // leaf_dev
    vmem = pl.BlockSpec(memory_space=pltpu.VMEM)
    hbm = pl.BlockSpec(memory_space=pl.ANY)
    dma = pltpu.SemaphoreType.DMA
    return pl.pallas_call(
        functools.partial(kernel, n),
        out_shape=jax.ShapeDtypeStruct(panels.shape, BF16),
        in_specs=[vmem, vmem, vmem, hbm, hbm, pl.BlockSpec(memory_space=pltpu.SMEM)],
        out_specs=vmem,
        scratch_shapes=[
            pltpu.VMEM((leaves, columns, points), BF16),
            pltpu.VMEM(near_blocks.shape, BF16),
            pltpu.VMEM(coupling.shape, BF16),
            pltpu.VMEM((leaf_dev * 8 * rank, 2 * rank), F32),
            pltpu.VMEM((min(leaves // 8, 27), 8 * half, 2 * rank * leaf_dev), BF16),
            pltpu.VMEM((min(leaves // 64, 27), 8 * half, 2 * rank), BF16),
            pltpu.VMEM((leaves * half, 2 * columns), BF16),
            pltpu.VMEM((group, half, 2 * columns), F32),
            pltpu.VMEM((n // group * half, 2 * columns), BF16),
            dma((leaf_dev * 3,)),
            dma,
            dma((27,)),
            dma((27,)),
            dma((n // 2,)),
            dma((n // 2,)),
            dma((n // 2,)),
            dma((n // 2,)),
            dma((group,)),
            dma((group,)),
            dma((n // group,)),
            dma((n // group,)),
        ],
        compiler_params=pltpu.CompilerParams(
            collective_id=0, has_side_effects=True, vmem_limit_bytes=60 * 2**20
        ),
    )(panels, basis, transfer, near_blocks, coupling, near_list)


def solution(mesh):
    placed = (
        P("leaf", None, None),
        P("leaf", None, None),
        P("leaf", None, None),
        P("leaf", None, None, None),
        P(),
        P("leaf", None),
    )
    return jax.shard_map(
        per_device, mesh=mesh, in_specs=placed, out_specs=P("leaf", None, None), check_vma=False
    )
```

profile of v0, /device:TPU:0, one launch (start us, length us, event | category | flops | bytes accessed | tf_op | source)
XLA Modules:
  0.0 25.9 jit_solution(8975640583852854730)
XLA Ops:
  0.0 24.4 %shard_map.64 = bf16[2,64,256]{2,1,0:T(8,128)(2,1)} custom-call(bf16[2,64,256]{2,1,0:T(8,128)(2,1)} %panels.1, bf16[2,64,256]{2,1,0:T(8,128)(2,1)} %basis.1, bf16[2,64,64]{2,1,0:T(8,128)(2,1)} %transfer.1, bf16[2,27,256,256]{3,2,1,0:T(8,128)(2,1)} %blocks_hbm.1, bf16[343,64,128]{2,1,0:T(8,128)(2,1)} %bitcast.7, s32[2,27]{1,0:T(2,128)} %near_list.1), custom_call_target="tpu_custom_call" | custom-call | tf_op jit(solution)/shard_map/pallas_call | solution.py:433
  24.4 1.5 %copy.9 = bf16[2,64,256]{2,1,0:T(8,128)(2,1)} copy(bf16[2,64,256]{2,1,0:T(8,128)(2,1)} %shard_map.64) | data formatting | bytes 131072
where the time goes:
time: 26.1 us; the launch traced here: 25.9 us
  Pallas kernels  24.4 us (93%)
  local copies, waits for them, and re-layouts  1.47 us (6%)
    pallas_call x1, Pallas kernels, per_device(): pl.pallas_call(functools.partial(kernel, n), out_shape=jax.ShapeDtypeStru...  24.4 us
    unnamed x1, local copies, waits for them, and re-layouts  1.47 us

commit v1 on v0

--- a/solution.py
+++ b/solution.py
@@ -188,6 +188,14 @@
     for l in range(leaf_dev):
         all_panels[me * leaf_dev + l] = panels[l]
 
+    mine = me // group
+    parent = coords_of(mine, axis_bits(0, bit_count - 3))
+    leaf_bits = axis_bits(0, bit_count)
+    targets = [coords_of(me * leaf_dev + l, leaf_bits) for l in range(leaf_dev)]
+    loads[0].wait()
+    far_mats([parent], bit_count - 3, coupling, 1, spread, mats1)
+    far_mats(targets, bit_count, coupling, 0, spread, mats0)
+
     pl.semaphore_wait(barrier, n - 1)
 
     def own_block(device):
@@ -319,7 +327,6 @@
 
     for j in range(1, group):
         part_copy(j).wait_recv()
-    mine = me // group
     total = parts[0]
     for j in range(1, group):
         total = total + parts[j]
@@ -355,13 +362,6 @@
         for k in range(1, places):
             coef_copy(j, k).wait_recv()
             relay_copy(j * places + k, coef_device(j, k)).start()
-
-    parent = coords_of(mine, axis_bits(0, bit_count - 3))
-    leaf_bits = axis_bits(0, bit_count)
-    targets = [coords_of(me * leaf_dev + l, leaf_bits) for l in range(leaf_dev)]
-    loads[0].wait()
-    far_mats([parent], bit_count - 3, coupling, 1, spread, mats1)
-    far_mats(targets, bit_count, coupling, 0, spread, mats0)
 
     @pl.loop(0, chips)
     def _(m):
@@ -432,7 +432,7 @@
     dma = pltpu.SemaphoreType.DMA
     return pl.pallas_call(
         functools.partial(kernel, n),
-        out_shape=jax.ShapeDtypeStruct(panels.shape, BF16),
+        out_shape=pltpu.VMEM(panels.shape, BF16),
         in_specs=[vmem, vmem, vmem, hbm, hbm, pl.BlockSpec(memory_space=pltpu.SMEM)],
         out_specs=vmem,
         scratch_shapes=[

time: 26.1 us -> 26.6 us (1.019)
  the two profiles are of different devices: /device:TPU:0 before, /device:TPU:1 now
where the time goes in v1:
time: 26.6 us; the launch traced here: 26.4 us
  Pallas kernels  25.8 us (97%)
  local copies, waits for them, and re-layouts  0.63 us (2%)
    pallas_call x1, Pallas kernels, per_device(): pl.pallas_call(functools.partial(kernel, n), out_shape=pltpu.VMEM(panels....  25.8 us
    unnamed x1, local copies, waits for them, and re-layouts  0.63 us

profile of v1, /device:TPU:1, one launch (start us, length us, event | category | flops | bytes accessed | tf_op | source)
XLA Modules:
  0.0 26.4 jit_solution(4161922195996309099)
XLA Ops:
  0.0 25.8 %shard_map.64 = bf16[2,64,256]{2,1,0:T(8,128)(2,1)S(1)} custom-call(bf16[2,64,256]{2,1,0:T(8,128)(2,1)} %panels.1, bf16[2,64,256]{2,1,0:T(8,128)(2,1)} %basis.1, bf16[2,64,64]{2,1,0:T(8,128)(2,1)} %transfer.1, bf16[2,27,256,256]{3,2,1,0:T(8,128)(2,1)} %blocks_hbm.1, bf16[343,64,128]{2,1,0:T(8,128)(2,1)} %bitcast.7, s32[2,27]{1,0:T(2,128)} %near_list.1), custom_call_target="tpu_custom_call" | custom-call | tf_op jit(solution)/shard_map/pallas_call | solution.py:433
  25.8 0.6 %copy.9 = bf16[2,64,256]{2,1,0:T(8,128)(2,1)} copy(bf16[2,64,256]{2,1,0:T(8,128)(2,1)S(1)} %shard_map.64) | data formatting | bytes 131072

commit v2 on v1

v2 whole, which is shorter than its diff:
```python
import functools

import jax
import jax.numpy as jnp
from jax import lax
from jax.experimental import pallas as pl
from jax.experimental.pallas import tpu as pltpu
from jax.sharding import PartitionSpec as P

MESH = pl.DeviceIdType.MESH
F32 = jnp.float32
BF16 = jnp.bfloat16
REACH = 3
SPAN = 2 * REACH + 1
TN = (((0,), (0,)), ((), ()))
NT = (((1,), (1,)), ((), ()))
COEFS, TERMS, CLUSTERS, SUMS = range(4)


def axis_bits(first, bit_count):
    return [[b for b in range(bit_count) if (b + first) % 3 == a] for a in range(3)]


def halved(index, times):
    return index // 2**times if isinstance(index, int) else lax.div(index, 2**times)


def bit_of(index, b):
    high = halved(index, b) if b else index
    return high % 2 if isinstance(index, int) else lax.rem(high, 2)


def coords_of(index, bits):
    return [
        sum(bit_of(index, b) * 2**p for p, b in enumerate(bits[a])) + index * 0 for a in range(3)
    ]


def index_of(coords, bits):
    return sum(bit_of(coords[a], p) * 2**b for a in range(3) for p, b in enumerate(bits[a]))


def inside(coords, bits):
    ok = None
    for a in range(3):
        here = (coords[a] >= 0) & (coords[a] < 2 ** len(bits[a]))
        ok = here if ok is None else ok & here
    return ok


def flipped(index, mask, bit_count):
    result = 0
    for b in range(bit_count):
        one, two = bit_of(index, b), bit_of(mask, b)
        result = result + (one + two - 2 * one * two) * 2**b
    return result


def extract(coupling, code, level, spread, at):
    half = coupling.shape[1] // 2
    spread[at : at + 2 * half, :] = coupling[code].astype(F32)
    return spread[pl.ds(at + level, half, stride=2), :].astype(BF16)


def code_of(d):
    return (SPAN * (d[0] + REACH) + d[1] + REACH) * SPAN + d[2] + REACH


def candidate(target, bit_count, i):
    bits = axis_bits(0, bit_count - 3)
    home = [c // 2 for c in target]
    if 2 ** (bit_count - 3) <= 27:
        upper = coords_of(i, bits)
        ok = None
        for a in range(3):
            near = jnp.abs(upper[a] - home[a]) <= 1
            ok = near if ok is None else ok & near
        return upper, i, ok
    upper = [home[0] + i // 9 - 1, home[1] + (i // 3) % 3 - 1, home[2] + i % 3 - 1]
    ok = inside(upper, bits)
    return upper, jnp.where(ok, index_of([jnp.maximum(u, 0) for u in upper], bits), 0), ok


def kernel(
    n,
    panels_hbm,
    basis_hbm,
    transfer_hbm,
    blocks_hbm,
    coupling_hbm,
    near_hbm,
    out,
    panels,
    basis,
    transfer,
    blocks,
    coupling,
    near_list,
    slot_of,
    spread,
    mats0,
    mats1,
    coefs,
    terms,
    clusters,
    kept,
    sent,
    sums,
    near,
    load_sem,
    panel_send,
    panel_recv,
    group_send,
    group_recv,
):
    leaf_dev, rank, points = basis.shape
    cols = panels.shape[1]
    slots = near_list.shape[1]
    shifts = coupling_hbm.shape[0]
    half = rank // 2
    low_bits = leaf_dev.bit_length() - 1
    dev_bits = n.bit_length() - 1
    bit_count = low_bits + dev_bits
    group = 8 // leaf_dev
    plane = min(8, n)
    plane_bits = plane.bit_length() - 1
    lines = n // plane
    teams = plane // group
    own_rows = leaf_dev * half
    me = lax.axis_index("leaf")
    line, spot = lax.div(me, plane), lax.rem(me, plane)

    loads = [
        pltpu.make_async_copy(source, target, load_sem.at[i])
        for i, (source, target) in enumerate(
            [
                (panels_hbm, panels.at[pl.ds(me * leaf_dev, leaf_dev)]),
                (basis_hbm, basis),
                (transfer_hbm, transfer),
                (near_hbm, near_list),
                (coupling_hbm, coupling.at[pl.ds(0, shifts)]),
                (blocks_hbm, blocks),
            ]
        )
    ]
    for load in loads[:5]:
        load.start()

    bits = axis_bits(low_bits, dev_bits)
    where = coords_of(me, bits)
    side = [1 - 2 * bit_of(c, 0) for c in where]
    kinds = [min(2 ** len(b), 3) for b in bits]

    def offset(a, kind):
        return side[a] * bit_of(kind, 0) - side[a] * halved(kind, 1)

    def moved(kind):
        there = [where[a] + offset(a, kind[a]) for a in range(3)]
        ok = inside(there, bits)
        return ok, jnp.where(ok, index_of([jnp.maximum(v, 0) for v in there], bits), me)

    def when(kind, ok, act):
        if all(k < 2 for k in kind):
            act()
        else:
            pl.when(ok)(act)

    def peer(r):
        return line * plane + flipped(spot, r, plane_bits)

    barrier = pltpu.get_barrier_semaphore()

    def greet(device):
        pl.semaphore_signal(barrier, inc=1, device_id=(device,), device_id_type=MESH)

    @pl.loop(1, lines)
    def _(j):
        greet(lax.rem(line + j, lines) * plane + spot)

    for r in range(1, plane):
        greet(peer(r))
    faces = [tuple(k if b == a else 0 for b in range(3)) for a in range(3) for k in range(1, kinds[a])]
    expected = lines - 1 + plane - 1
    for face in faces:
        ok, to = moved(face)
        when(face, ok, lambda: greet(to))
        expected = expected + jnp.where(ok, 1, 0)

    coupling[shifts] = jnp.zeros((rank, 2 * rank), BF16)

    for load in loads[:3]:
        load.wait()
    lane = lax.broadcasted_iota(jnp.int32, (half, 2 * cols), 1)

    def packed(value, at):
        spread[at : at + rank, :] = value
        even = spread[pl.ds(at, half, stride=2), :]
        odd = spread[pl.ds(at + 1, half, stride=2), :]
        return jnp.where(lane < cols, even, odd).astype(BF16)

    flats = []
    for l in range(leaf_dev):
        panel = panels[me * leaf_dev + l]
        flat = lax.dot_general(
            basis[l], jnp.concatenate([panel, panel], axis=0), NT, preferred_element_type=F32
        )
        at = pl.multiple_of(line * own_rows, own_rows) + l * half
        coefs[pl.ds(pl.multiple_of(at, half), half), :] = packed(flat, l * rank)
        flats.append(flat.astype(BF16))

    along_x, along_y, along_z = (range(1, k) for k in kinds)

    def search():
        loads[3].wait()

        @pl.loop(0, kinds[1] * kinds[2])
        def _(i):
            y, z = lax.div(i, kinds[2]), lax.rem(i, kinds[2])

            def find(l, leaf):
                total = 0
                for k in range(slots):
                    total = jnp.where(near_list[l, k] == leaf, k, total)
                return total

            _, device = moved((0, y, z))
            for l in range(leaf_dev):
                for m in range(leaf_dev):
                    slot_of[i, l * leaf_dev + m] = find(l, device * leaf_dev + m)
            for x in along_x:
                e = offset(0, x)
                _, device = moved((x, y, z))
                leaf = device * leaf_dev + halved(1 - e, 1)
                slot_of[i, leaf_dev * leaf_dev + x - 1] = find(halved(1 + e, 1), leaf)

    early = line * 2 < lines
    pl.when(early)(search)

    pl.semaphore_wait(barrier, expected)

    def line_copy(j, ref, rows, which):
        block = ref.at[pl.ds(pl.multiple_of(line * rows, rows), rows), :]
        return pltpu.make_async_remote_copy(
            src_ref=block,
            dst_ref=block,
            send_sem=group_send.at[which],
            recv_sem=group_recv.at[which],
            device_id=(lax.rem(line + j, lines) * plane + spot,),
            device_id_type=MESH,
        )

    def plane_copy(r, source, target, which):
        return pltpu.make_async_remote_copy(
            src_ref=source,
            dst_ref=target,
            send_sem=group_send.at[which],
            recv_sem=group_recv.at[which],
            device_id=(peer(r),),
            device_id_type=MESH,
        )

    def everything(which):
        whole = {
            COEFS: coefs.at[pl.ds(0, (lines - 1) * own_rows), :],
            TERMS: terms.at[pl.ds(1, plane - 1)],
            CLUSTERS: clusters.at[pl.ds(0, (lines - 1) * teams * half), :],
            SUMS: sums,
        }[which]
        return plane_copy(1, whole, whole, which)

    def panel_copy(kind, e, source, receiver):
        first, count = (0, leaf_dev) if kind[0] == 0 else (halved(1 - e, 1), 1)
        rows = panels.at[pl.ds(source * leaf_dev + first, count)]
        at = (kind[0] * kinds[1] + kind[1]) * kinds[2] + kind[2]
        return pltpu.make_async_remote_copy(
            src_ref=rows,
            dst_ref=rows,
            send_sem=panel_send.at[at],
            recv_sem=panel_recv.at[at],
            device_id=(receiver,),
            device_id_type=MESH,
        )

    def sends(kind, act):
        a = 1 if kind[1] else 0 if kind[0] else 2
        hop = tuple(k if b == a else 0 for b, k in enumerate(kind))
        rest = tuple(0 if b == a else k for b, k in enumerate(kind))
        ok, to = moved(hop)
        known, source = moved(rest)
        e = offset(0, kind[0]) * (-1 if a == 0 else 1)
        when(kind, ok & known, lambda: act(panel_copy(kind, e, source, to)))

    def receives(kind):
        known, source = moved(kind)
        copy = panel_copy(kind, offset(0, kind[0]), source, peer(1))
        when(kind, known, lambda: copy.wait_recv())

    def start(copy):
        copy.start()

    @pl.loop(1, lines)
    def _(j):
        line_copy(lines - j, coefs, own_rows, COEFS).start()

    for z in reversed(along_z):
        sends((0, 0, z), start)
    for x in along_x:
        sends((x, 0, 0), start)
    for y in reversed(along_y):
        sends((0, y, 0), start)

    term = None
    for l in range(leaf_dev):
        part = lax.dot_general(transfer[l], flats[l], TN, preferred_element_type=F32)
        term = part if term is None else term + part
    terms[0] = packed(term, leaf_dev * rank)

    for r in reversed(range(1, plane)):
        plane_copy(r, terms.at[0], terms.at[r], TERMS).start()

    loads[4].wait()
    loads[5].start()

    chunk = min(8 // leaf_dev, lines)
    chunks = lines // chunk
    mine = lax.div(me, group)
    parent = coords_of(mine, axis_bits(0, bit_count - 3))
    parents = bit_count - 3
    candidates = min(2 ** (parents - 3), 27)

    @pl.loop(0, candidates)
    def _(i):
        upper, _, ok = candidate(parent, parents, i)
        for h in range(8):
            d = [2 * upper[a] + (h >> a & 1) - parent[a] for a in range(3)]
            use = ok & ((jnp.abs(d[0]) > 1) | (jnp.abs(d[1]) > 1) | (jnp.abs(d[2]) > 1))
            code = jnp.where(use, code_of(d), shifts)
            mats1[i, h * half : (h + 1) * half, :] = extract(coupling, code, 1, spread, h * rank)

    here = coords_of(line * plane, bits)
    base = coords_of(spot, bits)

    def leaf_mats(c):
        for r in range(plane):
            goal = list(base)
            for a in range(3):
                for p, b in enumerate(bits[a]):
                    if b < plane_bits and r >> b & 1:
                        goal[a] = goal[a] + (1 - 2 * bit_of(spot, b)) * 2**p
            target = [here[a] + goal[a] for a in range(3)]
            for j in range(chunk):
                there = coords_of((c * chunk + j) * plane, bits)
                source = [there[a] + base[a] for a in range(3)]
                d = [source[a] - target[a] for a in range(3)]
                close = jnp.abs(d[0]) <= 1
                for a in (1, 2):
                    close = close & (jnp.abs(halved(source[a], 1) - halved(target[a], 1)) <= 1)
                apart = (jnp.abs(d[1]) > 1) | (jnp.abs(d[2]) > 1)
                parts = {}
                for e in range(1 - leaf_dev, leaf_dev):
                    dx = leaf_dev * d[0] + e
                    use = close & (apart | (jnp.abs(dx) > 1))
                    code = jnp.where(use, code_of([dx, d[1], d[2]]), shifts)
                    at = ((r % 2 * chunk + j) * (2 * leaf_dev - 1) + e + leaf_dev - 1) * rank
                    parts[e] = extract(coupling, code, 0, spread, at)
                for m in range(leaf_dev):
                    rows = slice((j * leaf_dev + m) * half, (j * leaf_dev + m + 1) * half)
                    for l in range(leaf_dev):
                        mats0[c * plane + r, rows, 2 * rank * l : 2 * rank * (l + 1)] = parts[m - l]

    if chunks == 1:
        leaf_mats(0)
    else:
        pl.loop(0, chunks)(leaf_mats)

    for x in along_x:
        receives((x, 0, 0))
        for y in reversed(along_y):
            sends((x, y, 0), start)
    receives((0, 0, 1))
    for x in along_x:
        sends((x, 0, 1), start)
    for y in reversed(along_y):
        sends((0, y, 1), start)

    pl.when(~early)(search)

    everything(TERMS).wait_recv()
    for t in range(teams):
        total = None
        for r in range(t * group, (t + 1) * group):
            part = terms[r].astype(F32)
            total = part if total is None else total + part
        at = (line * teams + flipped(lax.div(spot, group), t, teams.bit_length() - 1)) * half
        clusters[pl.ds(pl.multiple_of(at, half), half), :] = total.astype(BF16)

    @pl.loop(1, lines)
    def _(j):
        line_copy(lines - j, clusters, teams * half, CLUSTERS).start()

    for z in along_z:
        if z > 1:
            receives((0, 0, z))
            for x in along_x:
                sends((x, 0, z), start)
            for y in reversed(along_y):
                sends((0, y, z), start)

    everything(COEFS).wait_recv()
    wide = lax.broadcasted_iota(jnp.int32, (cols, 2 * rank), 1) < rank
    depth = chunk * own_rows
    for r in reversed(range(plane)):
        total = None
        for c in range(chunks):
            part = lax.dot_general(
                coefs[c * depth : (c + 1) * depth, :],
                mats0[c * plane + r],
                TN,
                preferred_element_type=F32,
            )
            total = part if total is None else total + part
        one, two = total[:, : 2 * rank], total[:, 2 * rank :]
        straight = jnp.where(wide, one[:cols], two[cols:])
        crossed = jnp.where(wide, two[:cols], one[cols:])
        result = straight + pltpu.roll(crossed, rank, 1)
        if r == 0:
            kept[...] = result
        else:
            sent[r - 1] = result.astype(BF16)
    for r in reversed(range(1, plane)):
        plane_copy(r, sent.at[r - 1], sums.at[r - 1], SUMS).start()

    for z in along_z:
        for x in along_x:
            receives((x, 0, z))
            for y in reversed(along_y):
                sends((x, y, z), start)

    loads[5].wait()

    def near_part(y):
        totals = [None] * leaf_dev
        outer = [None] * len(along_x)

        def add(old, panel, l, slot):
            part = jnp.dot(panel, blocks[l, slot], preferred_element_type=F32)
            return part if old is None else old + part

        for z in range(kinds[2]):
            at = y * kinds[2] + z
            ok, device = moved((0, y, z))
            for m in range(leaf_dev):
                panel = panels[device * leaf_dev + m]
                if y > 1 or z > 1:
                    panel = jnp.where(ok, panel, jnp.zeros_like(panel))
                for l in range(leaf_dev):
                    totals[l] = add(totals[l], panel, l, slot_of[at, l * leaf_dev + m])
            for x in along_x:
                e = offset(0, x)
                ok, device = moved((x, y, z))
                panel = panels[device * leaf_dev + halved(1 - e, 1)]
                if x > 1 or y > 1 or z > 1:
                    panel = jnp.where(ok, panel, jnp.zeros_like(panel))
                slot = slot_of[at, leaf_dev * leaf_dev + x - 1]
                outer[x - 1] = add(outer[x - 1], panel, halved(1 + e, 1), slot)
        for l in range(leaf_dev):
            near[l] = totals[l] if y == 0 else near[l] + totals[l]
        for x in along_x:
            l = halved(1 + offset(0, x), 1)
            near[l] = near[l] + outer[x - 1]

    near_part(0)

    if lines > 1:
        everything(CLUSTERS).wait_recv()

    def step(i, total):
        _, q, _ = candidate(parent, parents, i)
        rows = pl.ds(pl.multiple_of(q * 8 * half, 8 * half), 8 * half)
        return total + lax.dot_general(clusters[rows, :], mats1[i], TN, preferred_element_type=F32)

    total = lax.fori_loop(0, candidates, step, jnp.zeros((2 * cols, 2 * rank), F32))
    down = (total[:cols, :rank] + total[cols:, rank:]).astype(BF16)
    lower = [
        lax.dot_general(down, transfer[l], NT, preferred_element_type=F32) for l in range(leaf_dev)
    ]
    kept[...] = kept[...] + jnp.concatenate(lower, axis=1)

    for y in along_y:
        for x in range(kinds[0]):
            for z in range(kinds[2]):
                receives((x, y, z))
        near_part(y)

    every = [
        (x, y, z)
        for x in range(kinds[0])
        for y in range(kinds[1])
        for z in range(kinds[2])
        if x or y or z
    ]
    for kind in every:
        sends(kind, lambda copy: copy.wait_send())
    everything(COEFS).wait_send()
    everything(TERMS).wait_send()
    everything(CLUSTERS).wait_send()

    everything(SUMS).wait_recv()
    total = kept[...]
    for r in range(plane - 1):
        total = total + sums[r].astype(F32)
    total = total.astype(BF16).astype(F32)
    pair = jnp.concatenate([jnp.where(wide, total, 0.0), jnp.where(wide, 0.0, total)], axis=0)
    far = jnp.dot(
        pair.astype(BF16),
        basis[...].reshape(leaf_dev * rank, points),
        preferred_element_type=F32,
    )
    for l in range(leaf_dev):
        out[l] = (near[l] + far[l * cols : (l + 1) * cols]).astype(BF16)
    everything(SUMS).wait_send()


def per_device(panels, basis, transfer, near_blocks, coupling, near_list):
    n = lax.axis_size("leaf")
    leaf_dev, cols, points = panels.shape
    rank = basis.shape[1]
    slots = near_list.shape[1]
    shifts = coupling.shape[1]
    half = rank // 2
    leaves = n * leaf_dev
    coupling = coupling.transpose(1, 0, 2).reshape(shifts, 2, half, 2 * rank)
    coupling = coupling.transpose(0, 2, 1, 3).reshape(shifts, rank, 2 * rank)
    plane = min(8, n)
    lines = n // plane
    teams = plane * leaf_dev // 8
    chunk = min(8 // leaf_dev, lines)
    kinds = [min(2 ** len(b), 3) for b in axis_bits(leaf_dev.bit_length() - 1, n.bit_length() - 1)]
    faces = kinds[0] * kinds[1] * kinds[2]
    dma = pltpu.SemaphoreType.DMA
    return pl.pallas_call(
        functools.partial(kernel, n),
        out_shape=pltpu.VMEM(panels.shape, BF16),
        in_specs=[pl.BlockSpec(memory_space=pl.ANY)] * 6,
        out_specs=pl.BlockSpec(memory_space=pltpu.VMEM),
        scratch_shapes=[
            pltpu.VMEM((leaves, cols, points), BF16),
            pltpu.VMEM(basis.shape, BF16),
            pltpu.VMEM(transfer.shape, BF16),
            pltpu.VMEM(near_blocks.shape, BF16),
            pltpu.VMEM((shifts + 1, rank, 2 * rank), BF16),
            pltpu.SMEM(near_list.shape, jnp.int32),
            pltpu.SMEM((kinds[1] * kinds[2], leaf_dev * leaf_dev + 2), jnp.int32),
            pltpu.VMEM((max(2 * chunk * (2 * leaf_dev - 1), 8) * rank, 2 * rank), F32),
            pltpu.VMEM(
                (plane * (lines // chunk), chunk * leaf_dev * half, 2 * rank * leaf_dev), BF16
            ),
            pltpu.VMEM((min(leaves // 64, 27), 8 * half, 2 * rank), BF16),
            pltpu.VMEM((lines * leaf_dev * half, 2 * cols), BF16),
            pltpu.VMEM((plane, half, 2 * cols), BF16),
            pltpu.VMEM((lines * teams * half, 2 * cols), BF16),
            pltpu.VMEM((cols, leaf_dev * rank), F32),
            pltpu.VMEM((plane - 1, cols, leaf_dev * rank), BF16),
            pltpu.VMEM((plane - 1, cols, leaf_dev * rank), BF16),
            pltpu.VMEM((leaf_dev, cols, points), F32),
            dma((6,)),
            dma((faces,)),
            dma((faces,)),
            dma((4,)),
            dma((4,)),
        ],
        compiler_params=pltpu.CompilerParams(
            collective_id=0, has_side_effects=True, vmem_limit_bytes=60 * 2**20
        ),
    )(panels, basis, transfer, near_blocks, coupling, near_list)


def solution(mesh):
    placed = (
        P("leaf", None, None),
        P("leaf", None, None),
        P("leaf", None, None),
        P("leaf", None, None, None),
        P(),
        P("leaf", None),
    )
    return jax.shard_map(
        per_device, mesh=mesh, in_specs=placed, out_specs=P("leaf", None, None), check_vma=False
    )
```

time: 26.6 us -> 17.9 us (0.67)
  the two profiles are of different devices: /device:TPU:1 before, /device:TPU:0 now
where the time goes in v2:
time: 17.9 us; the launch traced here: 17.7 us
  Pallas kernels  17.1 us (96%)
  local copies, waits for them, and re-layouts  0.63 us (4%)
    pallas_call x1, Pallas kernels, per_device(): pl.pallas_call(functools.partial(kernel, n), out_shape=pltpu.VMEM(panels....  17.1 us
    unnamed x1, local copies, waits for them, and re-layouts  0.63 us

profile of v2, /device:TPU:0, one launch (start us, length us, event | category | flops | bytes accessed | tf_op | source)
XLA Modules:
  0.0 17.7 jit_solution(240783354407772872)
XLA Ops:
  0.0 17.1 %shard_map.64 = bf16[2,64,256]{2,1,0:T(8,128)(2,1)S(1)} custom-call(bf16[2,64,256]{2,1,0:T(8,128)(2,1)} %panels_hbm.1, bf16[2,64,256]{2,1,0:T(8,128)(2,1)} %basis_hbm.1, bf16[2,64,64]{2,1,0:T(8,128)(2,1)} %transfer_hbm.1, bf16[2,27,256,256]{3,2,1,0:T(8,128)(2,1)} %blocks_hbm.1, bf16[343,64,128]{2,1,0:T(8,128)(2,1)} %bitcast.7, s32[2,27]{1,0:T(2,128)} %near_hbm.1), custom_call_target="tpu_custom_call" | custom-call | tf_op jit(solution)/shard_map/pallas_call | solution.py:541
  17.1 0.6 %copy.9 = bf16[2,64,256]{2,1,0:T(8,128)(2,1)} copy(bf16[2,64,256]{2,1,0:T(8,128)(2,1)S(1)} %shard_map.64) | data formatting | bytes 131072

commit v3 on v2

--- a/solution.py
+++ b/solution.py
@@ -14,7 +14,7 @@
 SPAN = 2 * REACH + 1
 TN = (((0,), (0,)), ((), ()))
 NT = (((1,), (1,)), ((), ()))
-COEFS, TERMS, CLUSTERS, SUMS = range(4)
+COEFS, SUMS = range(2)
 
 
 def axis_bits(first, bit_count):
@@ -64,21 +64,6 @@
 
 def code_of(d):
     return (SPAN * (d[0] + REACH) + d[1] + REACH) * SPAN + d[2] + REACH
-
-
-def candidate(target, bit_count, i):
-    bits = axis_bits(0, bit_count - 3)
-    home = [c // 2 for c in target]
-    if 2 ** (bit_count - 3) <= 27:
-        upper = coords_of(i, bits)
-        ok = None
-        for a in range(3):
-            near = jnp.abs(upper[a] - home[a]) <= 1
-            ok = near if ok is None else ok & near
-        return upper, i, ok
-    upper = [home[0] + i // 9 - 1, home[1] + (i // 3) % 3 - 1, home[2] + i % 3 - 1]
-    ok = inside(upper, bits)
-    return upper, jnp.where(ok, index_of([jnp.maximum(u, 0) for u in upper], bits), 0), ok
 
 
 def kernel(
@@ -101,8 +86,7 @@
     mats0,
     mats1,
     coefs,
-    terms,
-    clusters,
+    reach,
     kept,
     sent,
     sums,
@@ -126,7 +110,7 @@
     plane_bits = plane.bit_length() - 1
     lines = n // plane
     teams = plane // group
-    own_rows = leaf_dev * half
+    own_rows = (leaf_dev + 1) * half
     me = lax.axis_index("leaf")
     line, spot = lax.div(me, plane), lax.rem(me, plane)
 
@@ -198,15 +182,22 @@
         odd = spread[pl.ds(at + 1, half, stride=2), :]
         return jnp.where(lane < cols, even, odd).astype(BF16)
 
+    def own_part(l):
+        return pl.ds(pl.multiple_of((line * (leaf_dev + 1) + l) * half, half), half)
+
     flats = []
     for l in range(leaf_dev):
         panel = panels[me * leaf_dev + l]
         flat = lax.dot_general(
             basis[l], jnp.concatenate([panel, panel], axis=0), NT, preferred_element_type=F32
         )
-        at = pl.multiple_of(line * own_rows, own_rows) + l * half
-        coefs[pl.ds(pl.multiple_of(at, half), half), :] = packed(flat, l * rank)
+        coefs[own_part(l), :] = packed(flat, l * rank)
         flats.append(flat.astype(BF16))
+    term = None
+    for l in range(leaf_dev):
+        part = lax.dot_general(transfer[l], flats[l], TN, preferred_element_type=F32)
+        term = part if term is None else term + part
+    coefs[own_part(leaf_dev), :] = packed(term, leaf_dev * rank)
 
     along_x, along_y, along_z = (range(1, k) for k in kinds)
 
@@ -238,13 +229,13 @@
 
     pl.semaphore_wait(barrier, expected)
 
-    def line_copy(j, ref, rows, which):
-        block = ref.at[pl.ds(pl.multiple_of(line * rows, rows), rows), :]
+    def line_copy(j):
+        block = coefs.at[pl.ds(pl.multiple_of(line * own_rows, own_rows), own_rows), :]
         return pltpu.make_async_remote_copy(
             src_ref=block,
             dst_ref=block,
-            send_sem=group_send.at[which],
-            recv_sem=group_recv.at[which],
+            send_sem=group_send.at[COEFS],
+            recv_sem=group_recv.at[COEFS],
             device_id=(lax.rem(line + j, lines) * plane + spot,),
             device_id_type=MESH,
         )
@@ -262,16 +253,22 @@
     def everything(which):
         whole = {
             COEFS: coefs.at[pl.ds(0, (lines - 1) * own_rows), :],
-            TERMS: terms.at[pl.ds(1, plane - 1)],
-            CLUSTERS: clusters.at[pl.ds(0, (lines - 1) * teams * half), :],
             SUMS: sums,
         }[which]
         return plane_copy(1, whole, whole, which)
 
-    def panel_copy(kind, e, source, receiver):
-        first, count = (0, leaf_dev) if kind[0] == 0 else (halved(1 - e, 1), 1)
+    front = halved(1 + side[0], 1)
+
+    def panel_copy(kind, lane, source, receiver):
+        first, count, late = 0, leaf_dev, 0
+        if kind[0]:
+            first, count = lane, 1
+        elif lane is not None:
+            first, count, late = (front, 1 - front)[lane], 1, lane
         rows = panels.at[pl.ds(source * leaf_dev + first, count)]
         at = (kind[0] * kinds[1] + kind[1]) * kinds[2] + kind[2]
+        if late:
+            at = kinds[0] * kinds[1] * kinds[2] + kind[1]
         return pltpu.make_async_remote_copy(
             src_ref=rows,
             dst_ref=rows,
@@ -281,18 +278,29 @@
             device_id_type=MESH,
         )
 
-    def sends(kind, act):
+    def lanes_of(kind):
+        return (0, 1) if kind[0] == 0 and kind[2] > 1 else (None,)
+
+    def hops_of(kind):
+        if kind[0] and kind[1] > 1 and kind[2] > 1:
+            return (kind[0], kind[1], 0)
         a = 1 if kind[1] else 0 if kind[0] else 2
-        hop = tuple(k if b == a else 0 for b, k in enumerate(kind))
-        rest = tuple(0 if b == a else k for b, k in enumerate(kind))
+        return tuple(k if b == a else 0 for b, k in enumerate(kind))
+
+    def sends(kind, act, lane=None):
+        hop = hops_of(kind)
+        rest = tuple(k - h for k, h in zip(kind, hop))
         ok, to = moved(hop)
         known, source = moved(rest)
-        e = offset(0, kind[0]) * (-1 if a == 0 else 1)
-        when(kind, ok & known, lambda: act(panel_copy(kind, e, source, to)))
-
-    def receives(kind):
+        if kind[0]:
+            lane = halved(1 + offset(0, kind[0]) * (1 if hop[0] else -1), 1)
+        when(kind, ok & known, lambda: act(panel_copy(kind, lane, source, to)))
+
+    def receives(kind, lane=None):
         known, source = moved(kind)
-        copy = panel_copy(kind, offset(0, kind[0]), source, peer(1))
+        if kind[0]:
+            lane = halved(1 - offset(0, kind[0]), 1)
+        copy = panel_copy(kind, lane, source, peer(1))
         when(kind, known, lambda: copy.wait_recv())
 
     def start(copy):
@@ -300,42 +308,41 @@
 
     @pl.loop(1, lines)
     def _(j):
-        line_copy(lines - j, coefs, own_rows, COEFS).start()
-
-    for z in reversed(along_z):
-        sends((0, 0, z), start)
+        line_copy(lines - j).start()
+
+    for lane in (0, 1):
+        for z in along_z:
+            if z > 1:
+                sends((0, 0, z), start, lane)
+    sends((0, 0, 1), start)
     for x in along_x:
         sends((x, 0, 0), start)
     for y in reversed(along_y):
         sends((0, y, 0), start)
 
-    term = None
-    for l in range(leaf_dev):
-        part = lax.dot_general(transfer[l], flats[l], TN, preferred_element_type=F32)
-        term = part if term is None else term + part
-    terms[0] = packed(term, leaf_dev * rank)
-
-    for r in reversed(range(1, plane)):
-        plane_copy(r, terms.at[0], terms.at[r], TERMS).start()
-
     loads[4].wait()
     loads[5].start()
 
     chunk = min(8 // leaf_dev, lines)
     chunks = lines // chunk
-    mine = lax.div(me, group)
-    parent = coords_of(mine, axis_bits(0, bit_count - 3))
     parents = bit_count - 3
-    candidates = min(2 ** (parents - 3), 27)
-
-    @pl.loop(0, candidates)
-    def _(i):
-        upper, _, ok = candidate(parent, parents, i)
-        for h in range(8):
-            d = [2 * upper[a] + (h >> a & 1) - parent[a] for a in range(3)]
-            use = ok & ((jnp.abs(d[0]) > 1) | (jnp.abs(d[1]) > 1) | (jnp.abs(d[2]) > 1))
-            code = jnp.where(use, code_of(d), shifts)
-            mats1[i, h * half : (h + 1) * half, :] = extract(coupling, code, 1, spread, h * rank)
+    parent_bits = axis_bits(0, parents)
+    team = lax.div(spot, group)
+
+    def parent_mats(c):
+        for t in range(teams):
+            goal = line * teams + flipped(team, t, teams.bit_length() - 1)
+            target = coords_of(goal, parent_bits)
+            for j in range(chunk):
+                source = coords_of((c * chunk + j) * teams + team, parent_bits)
+                d = [source[a] - target[a] for a in range(3)]
+                use = (jnp.abs(d[0]) > 1) | (jnp.abs(d[1]) > 1) | (jnp.abs(d[2]) > 1)
+                for a in range(3):
+                    use = use & (jnp.abs(halved(source[a], 1) - halved(target[a], 1)) <= 1)
+                code = jnp.where(use, code_of(d), shifts)
+                mat = extract(coupling, code, 1, spread, (t * chunk + j) * rank)
+                rows = slice(j * half, (j + 1) * half)
+                mats1[c, rows, 2 * rank * t : 2 * rank * (t + 1)] = mat
 
     here = coords_of(line * plane, bits)
     base = coords_of(spot, bits)
@@ -368,10 +375,18 @@
                     for l in range(leaf_dev):
                         mats0[c * plane + r, rows, 2 * rank * l : 2 * rank * (l + 1)] = parts[m - l]
 
-    if chunks == 1:
-        leaf_mats(0)
-    else:
-        pl.loop(0, chunks)(leaf_mats)
+    for build in (parent_mats, leaf_mats):
+        if chunks == 1:
+            build(0)
+        else:
+            pl.loop(0, chunks)(build)
+
+    reach[: leaf_dev * rank] = basis[...].reshape(leaf_dev * rank, points)
+    for l in range(leaf_dev):
+        lift = lax.dot_general(transfer[l], basis[l], TN, preferred_element_type=F32).astype(BF16)
+        for p in range(2):
+            at = (leaf_dev + 2 * l + p) * rank
+            reach[at : at + rank] = lift
 
     for x in along_x:
         receives((x, 0, 0))
@@ -385,60 +400,64 @@
 
     pl.when(~early)(search)
 
-    everything(TERMS).wait_recv()
-    for t in range(teams):
-        total = None
-        for r in range(t * group, (t + 1) * group):
-            part = terms[r].astype(F32)
-            total = part if total is None else total + part
-        at = (line * teams + flipped(lax.div(spot, group), t, teams.bit_length() - 1)) * half
-        clusters[pl.ds(pl.multiple_of(at, half), half), :] = total.astype(BF16)
-
-    @pl.loop(1, lines)
-    def _(j):
-        line_copy(lines - j, clusters, teams * half, CLUSTERS).start()
-
-    for z in along_z:
-        if z > 1:
-            receives((0, 0, z))
-            for x in along_x:
-                sends((x, 0, z), start)
-            for y in reversed(along_y):
-                sends((0, y, z), start)
-
     everything(COEFS).wait_recv()
     wide = lax.broadcasted_iota(jnp.int32, (cols, 2 * rank), 1) < rank
-    depth = chunk * own_rows
-    for r in reversed(range(plane)):
+    def gathered(c, first, count):
+        parts = []
+        for j in range(chunk):
+            at = (c * chunk + j) * own_rows + first * half
+            parts.append(coefs[at : at + count * half, :])
+        return jnp.concatenate(parts, axis=0)
+
+    def applied(first, count, mats, at):
         total = None
         for c in range(chunks):
             part = lax.dot_general(
-                coefs[c * depth : (c + 1) * depth, :],
-                mats0[c * plane + r],
-                TN,
-                preferred_element_type=F32,
+                gathered(c, first, count), mats[c * at[1] + at[0]], TN, preferred_element_type=F32
             )
             total = part if total is None else total + part
+        return total
+
+    low = lax.broadcasted_iota(jnp.int32, (half, 2 * rank), 1) < rank
+    every_down = applied(leaf_dev, 1, mats1, (0, 1))
+    for r in reversed(range(plane)):
+        total = applied(0, leaf_dev, mats0, (r, plane))
         one, two = total[:, : 2 * rank], total[:, 2 * rank :]
         straight = jnp.where(wide, one[:cols], two[cols:])
         crossed = jnp.where(wide, two[:cols], one[cols:])
         result = straight + pltpu.roll(crossed, rank, 1)
+        t = r // group
+        if r % group == group - 1:
+            one = every_down[:, 2 * rank * t : 2 * rank * (t + 1)]
+            straight = jnp.where(low, one[:half], one[cols + half :])
+            crossed = jnp.where(low, one[half:cols], one[cols : cols + half])
+            down = straight + pltpu.roll(crossed, rank, 1)
         if r == 0:
-            kept[...] = result
+            kept[:cols] = result
+            kept[cols:] = down
         else:
-            sent[r - 1] = result.astype(BF16)
+            sent[r - 1, :cols] = result.astype(BF16)
+            sent[r - 1, cols:] = down.astype(BF16)
     for r in reversed(range(1, plane)):
         plane_copy(r, sent.at[r - 1], sums.at[r - 1], SUMS).start()
 
-    for z in along_z:
-        for x in along_x:
-            receives((x, 0, z))
+    if kinds[2] > 2:
+        for lane in (0, 1):
+            receives((0, 0, 2), lane)
+            x = 1 + lane
+            if x in along_x:
+                sends((x, 0, 2), start)
+                if kinds[1] > 2:
+                    sends((x, 2, 2), start)
             for y in reversed(along_y):
-                sends((x, y, z), start)
-
-    loads[5].wait()
-
-    def near_part(y):
+                sends((0, y, 2), start, lane)
+
+    for x in along_x:
+        receives((x, 0, 1))
+        for y in reversed(along_y):
+            sends((x, y, 1), start)
+
+    def near_part(y, levels, first=False):
         totals = [None] * leaf_dev
         outer = [None] * len(along_x)
 
@@ -446,51 +465,52 @@
             part = jnp.dot(panel, blocks[l, slot], preferred_element_type=F32)
             return part if old is None else old + part
 
-        for z in range(kinds[2]):
+        for z in levels:
             at = y * kinds[2] + z
-            ok, device = moved((0, y, z))
+            _, device = moved((0, y, z))
             for m in range(leaf_dev):
                 panel = panels[device * leaf_dev + m]
-                if y > 1 or z > 1:
-                    panel = jnp.where(ok, panel, jnp.zeros_like(panel))
                 for l in range(leaf_dev):
                     totals[l] = add(totals[l], panel, l, slot_of[at, l * leaf_dev + m])
             for x in along_x:
                 e = offset(0, x)
                 ok, device = moved((x, y, z))
                 panel = panels[device * leaf_dev + halved(1 - e, 1)]
-                if x > 1 or y > 1 or z > 1:
+                if x > 1:
                     panel = jnp.where(ok, panel, jnp.zeros_like(panel))
                 slot = slot_of[at, leaf_dev * leaf_dev + x - 1]
                 outer[x - 1] = add(outer[x - 1], panel, halved(1 + e, 1), slot)
         for l in range(leaf_dev):
-            near[l] = totals[l] if y == 0 else near[l] + totals[l]
+            near[l] = totals[l] if first else near[l] + totals[l]
         for x in along_x:
             l = halved(1 + offset(0, x), 1)
             near[l] = near[l] + outer[x - 1]
 
-    near_part(0)
-
-    if lines > 1:
-        everything(CLUSTERS).wait_recv()
-
-    def step(i, total):
-        _, q, _ = candidate(parent, parents, i)
-        rows = pl.ds(pl.multiple_of(q * 8 * half, 8 * half), 8 * half)
-        return total + lax.dot_general(clusters[rows, :], mats1[i], TN, preferred_element_type=F32)
-
-    total = lax.fori_loop(0, candidates, step, jnp.zeros((2 * cols, 2 * rank), F32))
-    down = (total[:cols, :rank] + total[cols:, rank:]).astype(BF16)
-    lower = [
-        lax.dot_general(down, transfer[l], NT, preferred_element_type=F32) for l in range(leaf_dev)
-    ]
-    kept[...] = kept[...] + jnp.concatenate(lower, axis=1)
-
+    def near_when(y, levels):
+        for x in range(kinds[0]):
+            for z in levels:
+                if (x, y, z) not in taken:
+                    for lane in lanes_of((x, y, z)):
+                        receives((x, y, z), lane)
+        kind = (0, y, max(levels))
+        when(kind, moved(kind)[0], lambda: near_part(y, levels))
+
+    taken = [(x, 0, 1) for x in range(kinds[0])] + [(x, 0, 0) for x in range(kinds[0])]
+    taken += [(0, 0, 2)]
+    loads[5].wait()
+    near_part(0, range(2), first=True)
     for y in along_y:
-        for x in range(kinds[0]):
-            for z in range(kinds[2]):
-                receives((x, y, z))
-        near_part(y)
+        near_when(y, range(2))
+    if kinds[2] > 2:
+        for x in along_x:
+            receives((x, 0, 2))
+            sends((x, 1, 2), start)
+            taken.append((x, 0, 2))
+        near_when(0, [2])
+        near_when(1, [2])
+
+    if kinds[1] > 2 and kinds[2] > 2:
+        near_when(2, [2])
 
     every = [
         (x, y, z)
@@ -500,22 +520,26 @@
         if x or y or z
     ]
     for kind in every:
-        sends(kind, lambda copy: copy.wait_send())
+        for lane in lanes_of(kind):
+            sends(kind, lambda copy: copy.wait_send(), lane)
     everything(COEFS).wait_send()
-    everything(TERMS).wait_send()
-    everything(CLUSTERS).wait_send()
 
     everything(SUMS).wait_recv()
     total = kept[...]
     for r in range(plane - 1):
         total = total + sums[r].astype(F32)
-    total = total.astype(BF16).astype(F32)
-    pair = jnp.concatenate([jnp.where(wide, total, 0.0), jnp.where(wide, 0.0, total)], axis=0)
-    far = jnp.dot(
-        pair.astype(BF16),
-        basis[...].reshape(leaf_dev * rank, points),
-        preferred_element_type=F32,
+    leafs, down = total[:cols], total[cols:]
+    none = jnp.zeros_like(leafs)
+    down = jnp.concatenate([jnp.where(low, down, 0.0), jnp.where(low, 0.0, down)], axis=0)
+    pair = jnp.concatenate(
+        [
+            jnp.concatenate([jnp.where(wide, leafs, 0.0), jnp.where(wide, 0.0, leafs)], axis=0),
+            jnp.concatenate([down, none], axis=0),
+            jnp.concatenate([none, down], axis=0),
+        ],
+        axis=1,
     )
+    far = jnp.dot(pair.astype(BF16), reach[...], preferred_element_type=F32)
     for l in range(leaf_dev):
         out[l] = (near[l] + far[l * cols : (l + 1) * cols]).astype(BF16)
     everything(SUMS).wait_send()
@@ -536,7 +560,7 @@
     teams = plane * leaf_dev // 8
     chunk = min(8 // leaf_dev, lines)
     kinds = [min(2 ** len(b), 3) for b in axis_bits(leaf_dev.bit_length() - 1, n.bit_length() - 1)]
-    faces = kinds[0] * kinds[1] * kinds[2]
+    faces = kinds[0] * kinds[1] * kinds[2] + kinds[1]
     dma = pltpu.SemaphoreType.DMA
     return pl.pallas_call(
         functools.partial(kernel, n),
@@ -555,19 +579,18 @@
             pltpu.VMEM(
                 (plane * (lines // chunk), chunk * leaf_dev * half, 2 * rank * leaf_dev), BF16
             ),
-            pltpu.VMEM((min(leaves // 64, 27), 8 * half, 2 * rank), BF16),
-            pltpu.VMEM((lines * leaf_dev * half, 2 * cols), BF16),
-            pltpu.VMEM((plane, half, 2 * cols), BF16),
-            pltpu.VMEM((lines * teams * half, 2 * cols), BF16),
-            pltpu.VMEM((cols, leaf_dev * rank), F32),
-            pltpu.VMEM((plane - 1, cols, leaf_dev * rank), BF16),
-            pltpu.VMEM((plane - 1, cols, leaf_dev * rank), BF16),
+            pltpu.VMEM((lines // chunk, chunk * half, 2 * rank * teams), BF16),
+            pltpu.VMEM((lines * (leaf_dev + 1) * half, 2 * cols), BF16),
+            pltpu.VMEM((3 * leaf_dev * rank, points), BF16),
+            pltpu.VMEM((cols + half, leaf_dev * rank), F32),
+            pltpu.VMEM((plane - 1, cols + half, leaf_dev * rank), BF16),
+            pltpu.VMEM((plane - 1, cols + half, leaf_dev * rank), BF16),
             pltpu.VMEM((leaf_dev, cols, points), F32),
             dma((6,)),
             dma((faces,)),
             dma((faces,)),
-            dma((4,)),
-            dma((4,)),
+            dma((2,)),
+            dma((2,)),
         ],
         compiler_params=pltpu.CompilerParams(
             collective_id=0, has_side_effects=True, vmem_limit_bytes=60 * 2**20

time: 17.9 us -> 16.9 us (0.944)
  the two profiles are of different devices: /device:TPU:0 before, /device:TPU:3 now
where the time goes in v3:
time: 16.9 us; the launch traced here: 16.8 us
  Pallas kernels  16.1 us (95%)
  local copies, waits for them, and re-layouts  0.63 us (4%)
    pallas_call x1, Pallas kernels, per_device(): pl.pallas_call(functools.partial(kernel, n), out_shape=pltpu.VMEM(panels....  16.1 us
    unnamed x1, local copies, waits for them, and re-layouts  0.63 us

profile of v3, /device:TPU:3, one launch (start us, length us, event | category | flops | bytes accessed | tf_op | source)
XLA Modules:
  0.0 16.8 jit_solution(10132971585401645716)
XLA Ops:
  0.0 16.1 %shard_map.64 = bf16[2,64,256]{2,1,0:T(8,128)(2,1)S(1)} custom-call(bf16[2,64,256]{2,1,0:T(8,128)(2,1)} %panels_hbm.1, bf16[2,64,256]{2,1,0:T(8,128)(2,1)} %basis_hbm.1, bf16[2,64,64]{2,1,0:T(8,128)(2,1)} %transfer_hbm.1, bf16[2,27,256,256]{3,2,1,0:T(8,128)(2,1)} %blocks_hbm.1, bf16[343,64,128]{2,1,0:T(8,128)(2,1)} %bitcast.7, s32[2,27]{1,0:T(2,128)} %near_hbm.1), custom_call_target="tpu_custom_call" | custom-call | tf_op jit(solution)/shard_map/pallas_call | solution.py:565
  16.1 0.6 %copy.9 = bf16[2,64,256]{2,1,0:T(8,128)(2,1)} copy(bf16[2,64,256]{2,1,0:T(8,128)(2,1)S(1)} %shard_map.64) | data formatting | bytes 131072

commit v4 on v3

--- a/solution.py
+++ b/solution.py
@@ -14,7 +14,7 @@
 SPAN = 2 * REACH + 1
 TN = (((0,), (0,)), ((), ()))
 NT = (((1,), (1,)), ((), ()))
-COEFS, SUMS = range(2)
+COEFS, PAIR, SUMS = range(3)
 
 
 def axis_bits(first, bit_count):
@@ -88,6 +88,8 @@
     coefs,
     reach,
     kept,
+    pair_sent,
+    pair_in,
     sent,
     sums,
     near,
@@ -236,7 +238,7 @@
             dst_ref=block,
             send_sem=group_send.at[COEFS],
             recv_sem=group_recv.at[COEFS],
-            device_id=(lax.rem(line + j, lines) * plane + spot,),
+            device_id=(j * plane + spot,),
             device_id_type=MESH,
         )
 
@@ -253,11 +255,25 @@
     def everything(which):
         whole = {
             COEFS: coefs.at[pl.ds(0, (lines - 1) * own_rows), :],
+            PAIR: pair_in,
             SUMS: sums,
         }[which]
         return plane_copy(1, whole, whole, which)
 
     front = halved(1 + side[0], 1)
+
+    def semaphores(kind, late=0):
+        far = [int(k > 1) for k in kind]
+        if far[0]:
+            at = kind[1] * kinds[2] + kind[2]
+            return 4 + at, 10 + at
+        if kind[1]:
+            at = 4 + kind[1] + 2 * far[2]
+        elif kind[0]:
+            at = (1, 2, 9)[kind[2]]
+        else:
+            at = (0, 0, 3 + late)[kind[2]]
+        return 2 * far[1] + far[2], at
 
     def panel_copy(kind, lane, source, receiver):
         first, count, late = 0, leaf_dev, 0
@@ -266,14 +282,12 @@
         elif lane is not None:
             first, count, late = (front, 1 - front)[lane], 1, lane
         rows = panels.at[pl.ds(source * leaf_dev + first, count)]
-        at = (kind[0] * kinds[1] + kind[1]) * kinds[2] + kind[2]
-        if late:
-            at = kinds[0] * kinds[1] * kinds[2] + kind[1]
+        from_at, to_at = semaphores(kind, late)
         return pltpu.make_async_remote_copy(
             src_ref=rows,
             dst_ref=rows,
-            send_sem=panel_send.at[at],
-            recv_sem=panel_recv.at[at],
+            send_sem=panel_send.at[from_at],
+            recv_sem=panel_recv.at[to_at],
             device_id=(receiver,),
             device_id_type=MESH,
         )
@@ -282,7 +296,7 @@
         return (0, 1) if kind[0] == 0 and kind[2] > 1 else (None,)
 
     def hops_of(kind):
-        if kind[0] and kind[1] > 1 and kind[2] > 1:
+        if kind[0] and kind[1] > 1 and kind[2]:
             return (kind[0], kind[1], 0)
         a = 1 if kind[1] else 0 if kind[0] else 2
         return tuple(k if b == a else 0 for b, k in enumerate(kind))
@@ -296,24 +310,48 @@
             lane = halved(1 + offset(0, kind[0]) * (1 if hop[0] else -1), 1)
         when(kind, ok & known, lambda: act(panel_copy(kind, lane, source, to)))
 
-    def receives(kind, lane=None):
-        known, source = moved(kind)
-        if kind[0]:
-            lane = halved(1 - offset(0, kind[0]), 1)
-        copy = panel_copy(kind, lane, source, peer(1))
-        when(kind, known, lambda: copy.wait_recv())
+    def whole(count, from_at, to_at):
+        rows = panels.at[pl.ds(0, count)]
+        return pltpu.make_async_remote_copy(
+            src_ref=rows,
+            dst_ref=rows,
+            send_sem=panel_send.at[from_at],
+            recv_sem=panel_recv.at[to_at],
+            device_id=(peer(1),),
+            device_id_type=MESH,
+        )
+
+    def arrived(members, lane=None):
+        count = 0
+        for kind in members:
+            if kind[0] > 1:
+                single = whole(1, *semaphores(kind))
+                when(kind, moved(kind)[0], lambda: single.wait_recv())
+            else:
+                count += leaf_dev if kind[0] == 0 and lane is None else 1
+                from_at, to_at = semaphores(kind, lane or 0)
+                last = kind
+        if count:
+            copy = whole(count, from_at, to_at)
+            when(last, moved(last)[0], lambda: copy.wait_recv())
 
     def start(copy):
         copy.start()
 
-    @pl.loop(1, lines)
-    def _(j):
-        line_copy(lines - j).start()
-
-    for lane in (0, 1):
-        for z in along_z:
-            if z > 1:
-                sends((0, 0, z), start, lane)
+    def gather(first, last):
+        @pl.loop(first, last)
+        def _(j):
+            @pl.when(j != line)
+            def _():
+                line_copy(j).start()
+
+    gather(0, max(lines // 4, 1))
+    if kinds[2] > 2:
+        sends((0, 0, 2), start, 0)
+    gather(max(lines // 4, 1), lines)
+
+    if kinds[2] > 2:
+        sends((0, 0, 2), start, 1)
     sends((0, 0, 1), start)
     for x in along_x:
         sends((x, 0, 0), start)
@@ -389,12 +427,14 @@
             reach[at : at + rank] = lift
 
     for x in along_x:
-        receives((x, 0, 0))
+        arrived([(x, 0, 0)])
         for y in reversed(along_y):
             sends((x, y, 0), start)
-    receives((0, 0, 1))
+    arrived([(0, 0, 1)])
     for x in along_x:
         sends((x, 0, 1), start)
+        if kinds[1] > 2:
+            sends((x, 2, 1), start)
     for y in reversed(along_y):
         sends((0, y, 1), start)
 
@@ -420,30 +460,38 @@
 
     low = lax.broadcasted_iota(jnp.int32, (half, 2 * rank), 1) < rank
     every_down = applied(leaf_dev, 1, mats1, (0, 1))
-    for r in reversed(range(plane)):
+    downs = []
+    for t in range(teams):
+        one = every_down[:, 2 * rank * t : 2 * rank * (t + 1)]
+        straight = jnp.where(low, one[:half], one[cols + half :])
+        crossed = jnp.where(low, one[half:cols], one[cols : cols + half])
+        downs.append(straight + pltpu.roll(crossed, rank, 1))
+
+    def partial(r):
         total = applied(0, leaf_dev, mats0, (r, plane))
         one, two = total[:, : 2 * rank], total[:, 2 * rank :]
         straight = jnp.where(wide, one[:cols], two[cols:])
         crossed = jnp.where(wide, two[:cols], one[cols:])
-        result = straight + pltpu.roll(crossed, rank, 1)
-        t = r // group
-        if r % group == group - 1:
-            one = every_down[:, 2 * rank * t : 2 * rank * (t + 1)]
-            straight = jnp.where(low, one[:half], one[cols + half :])
-            crossed = jnp.where(low, one[half:cols], one[cols : cols + half])
-            down = straight + pltpu.roll(crossed, rank, 1)
-        if r == 0:
-            kept[:cols] = result
-            kept[cols:] = down
-        else:
-            sent[r - 1, :cols] = result.astype(BF16)
-            sent[r - 1, cols:] = down.astype(BF16)
-    for r in reversed(range(1, plane)):
-        plane_copy(r, sent.at[r - 1], sums.at[r - 1], SUMS).start()
+        return straight + pltpu.roll(crossed, rank, 1), downs[r // group]
+
+    for i in range(plane // 2):
+        result, down = partial(2 * i + 1)
+        pair_sent[i, :cols] = result.astype(BF16)
+        pair_sent[i, cols:] = down.astype(BF16)
+    plane_copy(1, pair_sent, pair_in, PAIR).start()
+    for i in range(plane // 2):
+        result, down = partial(2 * i)
+        kept[i, :cols] = result
+        kept[i, cols:] = down
+    everything(PAIR).wait_recv()
+    for i in reversed(range(1, plane // 2)):
+        sent[i - 1] = (kept[i] + pair_in[i].astype(F32)).astype(BF16)
+    for i in reversed(range(1, plane // 2)):
+        plane_copy(2 * i, sent.at[i - 1], sums.at[i - 1], SUMS).start()
 
     if kinds[2] > 2:
         for lane in (0, 1):
-            receives((0, 0, 2), lane)
+            arrived([(0, 0, 2)], lane)
             x = 1 + lane
             if x in along_x:
                 sends((x, 0, 2), start)
@@ -453,9 +501,8 @@
                 sends((0, y, 2), start, lane)
 
     for x in along_x:
-        receives((x, 0, 1))
-        for y in reversed(along_y):
-            sends((x, y, 1), start)
+        arrived([(x, 0, 1)])
+        sends((x, 1, 1), start)
 
     def near_part(y, levels, first=False):
         totals = [None] * leaf_dev
@@ -487,25 +534,19 @@
             near[l] = near[l] + outer[x - 1]
 
     def near_when(y, levels):
-        for x in range(kinds[0]):
-            for z in levels:
-                if (x, y, z) not in taken:
-                    for lane in lanes_of((x, y, z)):
-                        receives((x, y, z), lane)
+        if y:
+            arrived([(x, y, z) for x in range(kinds[0]) for z in levels])
         kind = (0, y, max(levels))
         when(kind, moved(kind)[0], lambda: near_part(y, levels))
 
-    taken = [(x, 0, 1) for x in range(kinds[0])] + [(x, 0, 0) for x in range(kinds[0])]
-    taken += [(0, 0, 2)]
     loads[5].wait()
     near_part(0, range(2), first=True)
     for y in along_y:
         near_when(y, range(2))
     if kinds[2] > 2:
         for x in along_x:
-            receives((x, 0, 2))
+            arrived([(x, 0, 2)])
             sends((x, 1, 2), start)
-            taken.append((x, 0, 2))
         near_when(0, [2])
         near_when(1, [2])
 
@@ -519,15 +560,23 @@
         for z in range(kinds[2])
         if x or y or z
     ]
+    for y in range(kinds[1] - 1):
+        for z in range(kinds[2] - 1):
+            mine = [k for k in every if k[0] < 2 and (k[1] > 1) == y and (k[2] > 1) == z]
+            last = mine[-1]
+            count = sum(1 if k[0] else leaf_dev for k in mine)
+            copy = whole(count, *semaphores(last))
+            when(last, moved((0,) + last[1:])[0], lambda: copy.wait_send())
     for kind in every:
-        for lane in lanes_of(kind):
-            sends(kind, lambda copy: copy.wait_send(), lane)
+        if kind[0] > 1:
+            sends(kind, lambda copy: copy.wait_send())
     everything(COEFS).wait_send()
+    everything(PAIR).wait_send()
 
     everything(SUMS).wait_recv()
-    total = kept[...]
-    for r in range(plane - 1):
-        total = total + sums[r].astype(F32)
+    total = kept[0] + pair_in[0].astype(F32)
+    for i in range(plane // 2 - 1):
+        total = total + sums[i].astype(F32)
     leafs, down = total[:cols], total[cols:]
     none = jnp.zeros_like(leafs)
     down = jnp.concatenate([jnp.where(low, down, 0.0), jnp.where(low, 0.0, down)], axis=0)
@@ -560,7 +609,7 @@
     teams = plane * leaf_dev // 8
     chunk = min(8 // leaf_dev, lines)
     kinds = [min(2 ** len(b), 3) for b in axis_bits(leaf_dev.bit_length() - 1, n.bit_length() - 1)]
-    faces = kinds[0] * kinds[1] * kinds[2] + kinds[1]
+    wider = kinds[1] * kinds[2] if kinds[0] > 2 else 0
     dma = pltpu.SemaphoreType.DMA
     return pl.pallas_call(
         functools.partial(kernel, n),
@@ -582,15 +631,17 @@
             pltpu.VMEM((lines // chunk, chunk * half, 2 * rank * teams), BF16),
             pltpu.VMEM((lines * (leaf_dev + 1) * half, 2 * cols), BF16),
             pltpu.VMEM((3 * leaf_dev * rank, points), BF16),
-            pltpu.VMEM((cols + half, leaf_dev * rank), F32),
-            pltpu.VMEM((plane - 1, cols + half, leaf_dev * rank), BF16),
-            pltpu.VMEM((plane - 1, cols + half, leaf_dev * rank), BF16),
+            pltpu.VMEM((plane // 2, cols + half, leaf_dev * rank), F32),
+            pltpu.VMEM((plane // 2, cols + half, leaf_dev * rank), BF16),
+            pltpu.VMEM((plane // 2, cols + half, leaf_dev * rank), BF16),
+            pltpu.VMEM((plane // 2 - 1, cols + half, leaf_dev * rank), BF16),
+            pltpu.VMEM((plane // 2 - 1, cols + half, leaf_dev * rank), BF16),
             pltpu.VMEM((leaf_dev, cols, points), F32),
             dma((6,)),
-            dma((faces,)),
-            dma((faces,)),
-            dma((2,)),
-            dma((2,)),
+            dma((4 + wider,)),
+            dma((10 + wider,)),
+            dma((3,)),
+            dma((3,)),
         ],
         compiler_params=pltpu.CompilerParams(
             collective_id=0, has_side_effects=True, vmem_limit_bytes=60 * 2**20

time: 16.9 us -> 16 us (0.947)
  Pallas kernels: 16.1 us -> 15.2 us
    pallas_call x1, Pallas kernels: 16.1 us -> 15.2 us  [per_device(): pl.pallas_call(functools.partial(kernel, n), out_shape=pltpu.VMEM(panels....]
where the time goes in v4:
time: 16 us; the launch traced here: 15.9 us
  Pallas kernels  15.2 us (95%)
  local copies, waits for them, and re-layouts  0.63 us (4%)
    pallas_call x1, Pallas kernels, per_device(): pl.pallas_call(functools.partial(kernel, n), out_shape=pltpu.VMEM(panels....  15.2 us
    unnamed x1, local copies, waits for them, and re-layouts  0.63 us

profile of v4, /device:TPU:3, one launch (start us, length us, event | category | flops | bytes accessed | tf_op | source)
XLA Modules:
  0.0 15.9 jit_solution(10289123799743488220)
XLA Ops:
  0.0 15.2 %shard_map.64 = bf16[2,64,256]{2,1,0:T(8,128)(2,1)S(1)} custom-call(bf16[2,64,256]{2,1,0:T(8,128)(2,1)} %panels_hbm.1, bf16[2,64,256]{2,1,0:T(8,128)(2,1)} %basis_hbm.1, bf16[2,64,64]{2,1,0:T(8,128)(2,1)} %transfer_hbm.1, bf16[2,27,256,256]{3,2,1,0:T(8,128)(2,1)} %blocks_hbm.1, bf16[343,64,128]{2,1,0:T(8,128)(2,1)} %bitcast.7, s32[2,27]{1,0:T(2,128)} %near_hbm.1), custom_call_target="tpu_custom_call" | custom-call | tf_op jit(solution)/shard_map/pallas_call | solution.py:614
  15.2 0.6 %copy.9 = bf16[2,64,256]{2,1,0:T(8,128)(2,1)} copy(bf16[2,64,256]{2,1,0:T(8,128)(2,1)S(1)} %shard_map.64) | data formatting | bytes 131072

commit v5 on v4

--- a/solution.py
+++ b/solution.py
@@ -296,7 +296,7 @@
         return (0, 1) if kind[0] == 0 and kind[2] > 1 else (None,)
 
     def hops_of(kind):
-        if kind[0] and kind[1] > 1 and kind[2]:
+        if kind[0] and kind[1] and (kind[1] > 1 or kind[2] > 1) and kind[2]:
             return (kind[0], kind[1], 0)
         a = 1 if kind[1] else 0 if kind[0] else 2
         return tuple(k if b == a else 0 for b, k in enumerate(kind))
@@ -438,7 +438,17 @@
     for y in reversed(along_y):
         sends((0, y, 1), start)
 
-    pl.when(~early)(search)
+    hurried = (line * 4 < lines) & (lax.rem(spot, 2) == 0)
+
+    def relay(lane):
+        arrived([(0, 0, 2)], lane)
+        x = 1 + lane
+        if x in along_x:
+            sends((x, 0, 2), start)
+            for y in reversed(along_y):
+                sends((x, y, 2), start)
+        for y in reversed(along_y):
+            sends((0, y, 2), start, lane)
 
     everything(COEFS).wait_recv()
     wide = lax.broadcasted_iota(jnp.int32, (cols, 2 * rank), 1) < rank
@@ -483,6 +493,8 @@
         result, down = partial(2 * i)
         kept[i, :cols] = result
         kept[i, cols:] = down
+    if kinds[2] > 2:
+        pl.when(~hurried)(lambda: relay(0))
     everything(PAIR).wait_recv()
     for i in reversed(range(1, plane // 2)):
         sent[i - 1] = (kept[i] + pair_in[i].astype(F32)).astype(BF16)
@@ -490,15 +502,8 @@
         plane_copy(2 * i, sent.at[i - 1], sums.at[i - 1], SUMS).start()
 
     if kinds[2] > 2:
-        for lane in (0, 1):
-            arrived([(0, 0, 2)], lane)
-            x = 1 + lane
-            if x in along_x:
-                sends((x, 0, 2), start)
-                if kinds[1] > 2:
-                    sends((x, 2, 2), start)
-            for y in reversed(along_y):
-                sends((0, y, 2), start, lane)
+        pl.when(hurried)(lambda: relay(0))
+        relay(1)
 
     for x in along_x:
         arrived([(x, 0, 1)])
@@ -539,14 +544,14 @@
         kind = (0, y, max(levels))
         when(kind, moved(kind)[0], lambda: near_part(y, levels))
 
+    pl.when(~early)(search)
     loads[5].wait()
     near_part(0, range(2), first=True)
-    for y in along_y:
+    for y in reversed(along_y):
         near_when(y, range(2))
     if kinds[2] > 2:
         for x in along_x:
             arrived([(x, 0, 2)])
-            sends((x, 1, 2), start)
         near_when(0, [2])
         near_when(1, [2])
 

time: 16 us -> 14.8 us (0.925)
  the two profiles are of different devices: /device:TPU:3 before, /device:TPU:0 now
where the time goes in v5:
time: 14.8 us; the launch traced here: 14.6 us
  Pallas kernels  14 us (95%)
  local copies, waits for them, and re-layouts  0.63 us (4%)
    pallas_call x1, Pallas kernels, per_device(): pl.pallas_call(functools.partial(kernel, n), out_shape=pltpu.VMEM(panels....  14 us
    unnamed x1, local copies, waits for them, and re-layouts  0.63 us

profile of v5, /device:TPU:0, one launch (start us, length us, event | category | flops | bytes accessed | tf_op | source)
XLA Modules:
  0.0 14.6 jit_solution(11323977638575336023)
XLA Ops:
  0.0 14.0 %shard_map.64 = bf16[2,64,256]{2,1,0:T(8,128)(2,1)S(1)} custom-call(bf16[2,64,256]{2,1,0:T(8,128)(2,1)} %panels_hbm.1, bf16[2,64,256]{2,1,0:T(8,128)(2,1)} %basis_hbm.1, bf16[2,64,64]{2,1,0:T(8,128)(2,1)} %transfer_hbm.1, bf16[2,27,256,256]{3,2,1,0:T(8,128)(2,1)} %blocks_hbm.1, bf16[343,64,128]{2,1,0:T(8,128)(2,1)} %bitcast.7, s32[2,27]{1,0:T(2,128)} %near_hbm.1), custom_call_target="tpu_custom_call" | custom-call | tf_op jit(solution)/shard_map/pallas_call | solution.py:619
  14.0 0.6 %copy.9 = bf16[2,64,256]{2,1,0:T(8,128)(2,1)} copy(bf16[2,64,256]{2,1,0:T(8,128)(2,1)S(1)} %shard_map.64) | data formatting | bytes 131072

commit v6 on v5

--- a/solution.py
+++ b/solution.py
@@ -553,10 +553,9 @@
         for x in along_x:
             arrived([(x, 0, 2)])
         near_when(0, [2])
+        if kinds[1] > 2:
+            near_when(2, [2])
         near_when(1, [2])
-
-    if kinds[1] > 2 and kinds[2] > 2:
-        near_when(2, [2])
 
     every = [
         (x, y, z)

time: 14.8 us -> 14.8 us (level)
  no operation moved by 1% of the time
where the time goes in v6:
time: 14.8 us; the launch traced here: 14.6 us
  Pallas kernels  14 us (95%)
  local copies, waits for them, and re-layouts  0.63 us (4%)
    pallas_call x1, Pallas kernels, per_device(): pl.pallas_call(functools.partial(kernel, n), out_shape=pltpu.VMEM(panels....  14 us
    unnamed x1, local copies, waits for them, and re-layouts  0.63 us

profile of v6, /device:TPU:0, one launch (start us, length us, event | category | flops | bytes accessed | tf_op | source)
XLA Modules:
  0.0 14.6 jit_solution(3573828369117239978)
XLA Ops:
  0.0 14.0 %shard_map.64 = bf16[2,64,256]{2,1,0:T(8,128)(2,1)S(1)} custom-call(bf16[2,64,256]{2,1,0:T(8,128)(2,1)} %panels_hbm.1, bf16[2,64,256]{2,1,0:T(8,128)(2,1)} %basis_hbm.1, bf16[2,64,64]{2,1,0:T(8,128)(2,1)} %transfer_hbm.1, bf16[2,27,256,256]{3,2,1,0:T(8,128)(2,1)} %blocks_hbm.1, bf16[343,64,128]{2,1,0:T(8,128)(2,1)} %bitcast.7, s32[2,27]{1,0:T(2,128)} %near_hbm.1), custom_call_target="tpu_custom_call" | custom-call | tf_op jit(solution)/shard_map/pallas_call | solution.py:618
  14.0 0.6 %copy.9 = bf16[2,64,256]{2,1,0:T(8,128)(2,1)} copy(bf16[2,64,256]{2,1,0:T(8,128)(2,1)S(1)} %shard_map.64) | data formatting | bytes 131072
